TPU v7x, 32 devices: a whole 2x2x4 slice. The times are simulated.
32 devices in a mesh: fsdp: 8 (over y, x, core), tp: 4 (over z).
Axes of the slice: x: 2, y: 2, z: 4, core: 2. Of those that a mesh axis runs over, the one named last changes fastest.
Arguments:
- tokens: bfloat16 [8192, 1536], P(('fsdp', 'tp')), may hold values from -6 to 6
- cotangent: bfloat16 [8192, 1536], P(('fsdp', 'tp')), may hold values from -6 to 6
- seq_start: int32 [32], P('fsdp'), may hold values from 0 to 1, as said below
- token_valid: int32 [8192], P('fsdp'), may hold values from 0 to 1, as said below
- norm_gain: float32 [1536], replicated, may hold values from 0.5 to 1.5
- proj_z: bfloat16 [1536, 3072], P('fsdp', 'tp'), may hold values from -0.15625 to 0.15625
- proj_x: bfloat16 [1536, 3072], P('fsdp', 'tp'), may hold values from -0.15625 to 0.15625
- proj_bc: bfloat16 [1536, 256], P('fsdp'), may hold values from -0.15625 to 0.15625
- proj_dt: bfloat16 [1536, 48], P('fsdp', 'tp'), may hold values from -0.15625 to 0.15625
- conv_chan: float32 [4, 3072], P(None, 'tp'), may hold values from -3 to 3
- bias_chan: float32 [3072], P('tp'), may hold values from -0.5 to 0.5
- conv_shared: float32 [4, 256], replicated, may hold values from -3 to 3
- bias_shared: float32 [256], replicated, may hold values from -0.5 to 0.5
- a_log: float32 [48], P('tp'), may hold values from -1 to 1.5
- dt_bias: float32 [48], P('tp'), may hold values from -8 to -2
- skip_gain: float32 [48], P('tp'), may hold values from 0.5 to 1.5
- gate_gain: float32 [3072], P('tp'), may hold values from 0.5 to 1.5
- proj_out: bfloat16 [3072, 1536], P('tp', 'fsdp'), may hold values from -0.109375 to 0.109375
Outputs:
- output: bfloat16 [8192, 1536], P(('fsdp', 'tp'))
- grad_tokens: bfloat16 [8192, 1536], P(('fsdp', 'tp'))
- grad_norm_gain: float32 [1536], replicated
- grad_proj_z: float32 [1536, 3072], P('fsdp', 'tp')
- grad_proj_x: float32 [1536, 3072], P('fsdp', 'tp')
- grad_proj_bc: float32 [1536, 256], P('fsdp')
- grad_proj_dt: float32 [1536, 48], P('fsdp', 'tp')
- grad_conv_chan: float32 [4, 3072], P(None, 'tp')
- grad_bias_chan: float32 [3072], P('tp')
- grad_conv_shared: float32 [4, 256], replicated
- grad_bias_shared: float32 [256], replicated
- grad_a_log: float32 [48], P('tp')
- grad_dt_bias: float32 [48], P('tp')
- grad_skip_gain: float32 [48], P('tp')
- grad_gate_gain: float32 [3072], P('tp')
- grad_proj_out: float32 [3072, 1536], P('tp', 'fsdp')
Inputs may be any that keep to these rules, and one draw needn't show every extreme that they name: `seq_start`: each buffer of 4 blocks has 1 at its first block; a sequence spans 4 to min(15, 4) blocks and no sequence crosses a buffer; after a buffer's last sequence the flags are 0; some buffer is filled with sequences to its end. `token_valid`: within a sequence all tokens are 1 except between 0 and 127 tokens at the end of its last block; every token of the blocks after a buffer's last sequence is 0.
All inputs are finite; a program needn't handle non-finite values.
Results may differ from a plain program's by a relative error of at most 0.02.
Values may be sent and summed in bfloat16 or wider, within the bound.
A program may use at most 192 MiB of HBM per device.

v0:
```python
import jax
import jax.numpy as jnp
from jax import lax
from jax.sharding import PartitionSpec as P

HEAD = 64
STATE = 128
STRETCH = 256
INNER = 3072
EPSILON = 1e-05
PRECISE = lax.Precision.HIGHEST


def causal_conv(signal, kernel, offset_bias, openings):
    length = signal.shape[0]
    tap_count = kernel.shape[0]
    padded = jnp.concatenate(
        [jnp.zeros((tap_count - 1, signal.shape[1]), jnp.float32), signal], axis=0
    )
    within = jnp.arange(length) % STRETCH
    opening = jnp.repeat(openings, STRETCH)
    result = jnp.zeros_like(signal) + offset_bias[None, :]
    for tap_index in range(tap_count):
        reach_back = tap_count - 1 - tap_index
        allowed = 1.0 - opening * (within < reach_back).astype(jnp.float32)
        result = (
            result
            + allowed[:, None] * padded[tap_index : tap_index + length] * kernel[tap_index][None, :]
        )
    return jax.nn.silu(result)


def state_scan(inputs, step_rates, decay_a, shared_b, shared_c, openings):
    seq_len, head_count, head_size = inputs.shape
    block_count = seq_len // STRETCH
    blocks_x = inputs.reshape(block_count, STRETCH, head_count, head_size)
    blocks_dt = step_rates.reshape(block_count, STRETCH, head_count)
    blocks_b = shared_b.reshape(block_count, STRETCH, shared_b.shape[1])
    blocks_c = shared_c.reshape(block_count, STRETCH, shared_c.shape[1])
    log_decay = blocks_dt * decay_a[None, None, :]
    lower = (jnp.arange(STRETCH)[:, None] >= jnp.arange(STRETCH)[None, :]).astype(jnp.float32)
    cumulative = jnp.einsum("ts,csh->cth", lower, log_decay, precision=PRECISE)
    spread = cumulative[:, :, None, :] - cumulative[:, None, :, :]
    weights = jnp.exp(jnp.where(lower[None, :, :, None] > 0, spread, -1e30))
    intersection = jnp.einsum("ctn,csn->cts", blocks_c, blocks_b, precision=PRECISE)
    scaled_x = blocks_x * blocks_dt[..., None]
    within_block = jnp.einsum(
        "ctsh,cshp->cthp", weights * intersection[..., None], scaled_x, precision=PRECISE
    )
    to_end = jnp.exp(cumulative[:, -1:, :] - cumulative)
    block_states = jnp.einsum(
        "cshp,csn->chpn", scaled_x * to_end[..., None], blocks_b, precision=PRECISE
    )
    carry_decay = jnp.exp(cumulative[:, -1, :])

    def advance(carried, block_item):
        opening, factor, fresh_state = block_item
        entering = carried * (1.0 - opening)
        return (entering * factor[:, None, None] + fresh_state, entering)

    initial = jnp.zeros((head_count, head_size, blocks_b.shape[-1]), jnp.float32)
    _, entering = lax.scan(advance, initial, (openings, carry_decay, block_states))
    across_block = (
        jnp.einsum("ctn,chpn->cthp", blocks_c, entering, precision=PRECISE)
        * jnp.exp(cumulative)[..., None]
    )
    return (within_block + across_block).reshape(seq_len, head_count, head_size)


def gated_branch(
    pre_z,
    pre_x,
    pre_bc,
    pre_dt,
    conv_chan,
    bias_chan,
    conv_shared,
    bias_shared,
    a_log,
    dt_bias,
    skip_gain,
    validity,
    openings,
):
    length = pre_x.shape[0]
    head_count = pre_dt.shape[1]
    features = causal_conv(pre_x, conv_chan, bias_chan, openings)
    shared = causal_conv(pre_bc, conv_shared, bias_shared, openings)
    step_rates = jax.nn.softplus(pre_dt + dt_bias[None, :]) * validity[:, None]
    decay_a = -jnp.exp(a_log)
    heads_x = features.reshape(length, head_count, HEAD)
    mixed_out = state_scan(
        heads_x, step_rates, decay_a, shared[:, :STATE], shared[:, STATE:], openings
    )
    mixed_out = mixed_out + skip_gain[None, :, None] * heads_x
    return mixed_out.reshape(length, head_count * HEAD) * jax.nn.silu(pre_z) * validity[:, None]


def shards(
    tokens,
    cotangent,
    seq_start,
    token_valid,
    norm_gain,
    proj_z,
    proj_x,
    proj_bc,
    proj_dt,
    conv_chan,
    bias_chan,
    conv_shared,
    bias_shared,
    a_log,
    dt_bias,
    skip_gain,
    gate_gain,
    proj_out,
):
    validity = token_valid.astype(jnp.float32)
    openings = seq_start.astype(jnp.float32)
    whole_z, whole_x, whole_bc, whole_dt, whole_out = (
        lax.all_gather(proj_z, "fsdp", axis=0, tiled=True),
        lax.all_gather(proj_x, "fsdp", axis=0, tiled=True),
        lax.all_gather(proj_bc, "fsdp", axis=0, tiled=True),
        lax.all_gather(proj_dt, "fsdp", axis=0, tiled=True),
        lax.all_gather(proj_out, "fsdp", axis=1, tiled=True),
    )
    resid = tokens.astype(jnp.float32)
    rstd = lax.rsqrt(jnp.mean(resid * resid, axis=1, keepdims=True) + EPSILON)
    normed = (resid * rstd * norm_gain[None, :]).astype(jnp.bfloat16)
    normed_all = lax.all_gather(normed, "tp", axis=0, tiled=True)
    pre_z = jnp.dot(normed_all, whole_z, preferred_element_type=jnp.float32)
    pre_x = jnp.dot(normed_all, whole_x, preferred_element_type=jnp.float32)
    pre_bc = jnp.dot(normed_all, whole_bc, preferred_element_type=jnp.float32)
    pre_dt = jnp.dot(normed_all, whole_dt, preferred_element_type=jnp.float32)

    def mixer(
        in_z,
        in_x,
        in_bc,
        in_dt,
        taps_chan,
        offset_chan,
        taps_shared,
        offset_shared,
        log_rate,
        step_bias,
        direct_gain,
    ):
        return gated_branch(
            in_z,
            in_x,
            in_bc,
            in_dt,
            taps_chan,
            offset_chan,
            taps_shared,
            offset_shared,
            log_rate,
            step_bias,
            direct_gain,
            validity,
            openings,
        )

    gated, mixer_back = jax.vjp(
        mixer,
        pre_z,
        pre_x,
        pre_bc,
        pre_dt,
        conv_chan,
        bias_chan,
        conv_shared,
        bias_shared,
        a_log,
        dt_bias,
        skip_gain,
    )
    squares = lax.psum(jnp.sum(gated * gated, axis=1), "tp")
    gate_rstd = lax.rsqrt(squares / INNER + EPSILON)[:, None]
    gnormed = (gated * gate_rstd * gate_gain[None, :]).astype(jnp.bfloat16)
    mixed = lax.psum_scatter(
        jnp.dot(gnormed, whole_out, preferred_element_type=jnp.float32).astype(jnp.bfloat16),
        "tp",
        scatter_dimension=0,
        tiled=True,
    ).astype(jnp.float32)
    cot_all = lax.all_gather(cotangent, "tp", axis=0, tiled=True)
    d_gnormed = jnp.einsum("td,cd->tc", cot_all, whole_out, preferred_element_type=jnp.float32)
    grad_out_rows = jnp.einsum("tc,td->cd", gnormed, cot_all, preferred_element_type=jnp.float32)
    output = (resid + mixed).astype(jnp.bfloat16)
    scaled = gate_gain[None, :] * d_gnormed
    d_gate_gain = jnp.sum(d_gnormed * gated * gate_rstd, axis=0)
    cross = lax.psum(jnp.sum(scaled * gated, axis=1), "tp")
    d_gated = (
        gate_rstd * scaled - gated * (gate_rstd * gate_rstd * gate_rstd) * (cross / INNER)[:, None]
    )
    grads = mixer_back(d_gated)
    grad_z = grads[0].astype(jnp.bfloat16)
    grad_x = grads[1].astype(jnp.bfloat16)
    grad_bc = grads[2].astype(jnp.bfloat16)
    grad_dt = grads[3].astype(jnp.bfloat16)
    weight_z = jnp.einsum("td,tc->dc", normed_all, grad_z, preferred_element_type=jnp.float32)
    weight_x = jnp.einsum("td,tc->dc", normed_all, grad_x, preferred_element_type=jnp.float32)
    weight_bc = jnp.einsum("td,tc->dc", normed_all, grad_bc, preferred_element_type=jnp.float32)
    weight_dt = jnp.einsum("td,tc->dc", normed_all, grad_dt, preferred_element_type=jnp.float32)

    def partial_term(grad_rows, weight_full):
        return jnp.einsum("tc,dc->td", grad_rows, weight_full, preferred_element_type=jnp.float32)

    d_normed = lax.psum_scatter(
        (
            partial_term(grad_z, whole_z)
            + partial_term(grad_x, whole_x)
            + partial_term(grad_bc, whole_bc)
            + partial_term(grad_dt, whole_dt)
        ).astype(jnp.bfloat16),
        "tp",
        scatter_dimension=0,
        tiled=True,
    ).astype(jnp.float32)
    owned_z, owned_x, owned_bc, owned_dt, owned_out = (
        lax.psum_scatter(
            weight_z.astype(jnp.bfloat16), "fsdp", scatter_dimension=0, tiled=True
        ).astype(jnp.float32),
        lax.psum_scatter(
            weight_x.astype(jnp.bfloat16), "fsdp", scatter_dimension=0, tiled=True
        ).astype(jnp.float32),
        lax.psum_scatter(
            weight_bc.astype(jnp.bfloat16), "fsdp", scatter_dimension=0, tiled=True
        ).astype(jnp.float32),
        lax.psum_scatter(
            weight_dt.astype(jnp.bfloat16), "fsdp", scatter_dimension=0, tiled=True
        ).astype(jnp.float32),
        lax.psum_scatter(
            grad_out_rows.astype(jnp.bfloat16), "fsdp", scatter_dimension=1, tiled=True
        ).astype(jnp.float32),
    )
    d_norm_gain = jnp.sum(d_normed * resid * rstd, axis=0)
    scaled_in = d_normed * norm_gain[None, :]
    d_resid = rstd * scaled_in - resid * (rstd * rstd * rstd) * jnp.mean(
        scaled_in * resid, axis=1, keepdims=True
    )
    grad_tokens = (d_resid + cotangent.astype(jnp.float32)).astype(jnp.bfloat16)
    summed = lax.psum(
        (
            grads[4],
            grads[5],
            grads[6],
            grads[7],
            grads[8],
            grads[9],
            grads[10],
            d_gate_gain,
            d_norm_gain,
        ),
        "fsdp",
    )
    shared_sums = (
        lax.psum(owned_bc.astype(jnp.bfloat16), "tp").astype(jnp.float32),
        lax.psum(summed[2].astype(jnp.bfloat16), "tp").astype(jnp.float32),
        lax.psum(summed[3].astype(jnp.bfloat16), "tp").astype(jnp.float32),
        lax.psum(summed[8].astype(jnp.bfloat16), "tp").astype(jnp.float32),
    )
    return (
        output,
        grad_tokens,
        shared_sums[3],
        owned_z,
        owned_x,
        shared_sums[0],
        owned_dt,
        summed[0],
        summed[1],
        shared_sums[1],
        shared_sums[2],
        summed[4],
        summed[5],
        summed[6],
        summed[7],
        owned_out,
    )


def solution(mesh):
    in_specs = (
        P(("fsdp", "tp"), None),
        P(("fsdp", "tp"), None),
        P("fsdp"),
        P("fsdp"),
        P(),
        P("fsdp", "tp"),
        P("fsdp", "tp"),
        P("fsdp", None),
        P("fsdp", "tp"),
        P(None, "tp"),
        P("tp"),
        P(),
        P(),
        P("tp"),
        P("tp"),
        P("tp"),
        P("tp"),
        P("tp", "fsdp"),
    )
    out_specs = (
        P(("fsdp", "tp"), None),
        P(("fsdp", "tp"), None),
        P(),
        P("fsdp", "tp"),
        P("fsdp", "tp"),
        P("fsdp", None),
        P("fsdp", "tp"),
        P(None, "tp"),
        P("tp"),
        P(),
        P(),
        P("tp"),
        P("tp"),
        P("tp"),
        P("tp"),
        P("tp", "fsdp"),
    )
    return jax.shard_map(shards, mesh=mesh, in_specs=in_specs, out_specs=out_specs, check_vma=False)
```

profile of v0, /device:TPU:0, one launch (start us, length us, event | category | flops | bytes accessed | tf_op | source)
XLA Modules:
  0.0 749.7 jit_solution(2506165639398660441)
XLA Ops:
  16.0 10.7 %all-gather = bf16[8,192,12]{1,2,0:T(8,128)(2,1)S(1)} all-gather(bf16[1,192,12]{1,2,0:T(8,128)(2,1)S(1)} %bitcast.207), channel_id=1, replica_groups=mesh['fsdp'=8,'tp'=4] {'fsdp'}, dimensions={0}, use_global_device_ids=true | all-gather | bytes 41472 | tf_op jit(solution)/shard_map/all_gather | solution.py:125
  26.9 10.4 %all_gather.24 = bf16[1536,256]{1,0:T(8,128)(2,1)S(1)} all-gather(bf16[192,256]{1,0:T(8,128)(2,1)S(1)} %copy-done.48), channel_id=1, replica_groups=mesh['fsdp'=8,'tp'=4] {'fsdp'}, dimensions={0}, use_global_device_ids=true | all-gather | bytes 884736 | tf_op jit(solution)/shard_map/all_gather | solution.py:124
  37.2 41.2 %all-gather.7.cloned.1.call-done = bf16[1024,1536]{1,0:T(8,128)(2,1)} async-done(((bf16[256,1536]{1,0:T(8,128)(2,1)}), bf16[1024,1536]{1,0:T(8,128)(2,1)}) %all-gather.7.cloned.1.call-update) | async-done | bytes 3145744 | tf_op jit(solution)/shard_map/all_gather | solution.py:131
  78.5 3.4 fusion.95
  82.6 2.9 fusion.121
  87.6 20.3 %all-gather.9.cloned.1.call-done = bf16[1536,768]{1,0:T(8,128)(2,1)} async-done(((bf16[192,768]{1,0:T(8,128)(2,1)}), bf16[1536,768]{1,0:T(8,128)(2,1)}) %all-gather.9.cloned.1.call-update) | async-done | bytes 2359312 | tf_op jit(solution)/shard_map/all_gather | solution.py:123
  107.9 5.2 fusion.120
  113.2 4.7 fusion.32
  117.9 3.6 copy.88
  121.5 5.1 reshape.258
  128.5 6.2 fusion.38
  134.9 14.7 %while.36 = (s32[]{:T(128)}, f32[12,64,128]{2,1,0:T(8,128)S(1)}, f32[4,12,64,128]{3,2,1,0:T(8,128)S(1)}, f32[4]{0:T(128)S(1)}, f32[4,12,1,1]{1,3,2,0:T(1,128)}, ...) while((s32[]{:T(128)}, f32[12,64,128]{2,1,0:T(8,128)S(1)}, ...), condition=%wide.region_2.3_spmd.clone, body=%wide.region_1.2_spmd.clone.sunk | while | flops 589828 | bytes 1967464 | solution.py:62
  152.4 14.1 %bitcast_add_fusion.3 = f32[4,256,12,64]{1,3,2,0:T(8,128)S(1)} fusion(f32[4,256,12,64]{1,3,2,0:T(8,128)S(1)} %fusion.123, f32[4,256,256]{2,1,0:T(8,128)S(1)} %copy-done.31, f32[4,256,12]{1,2,0:T(8,128)S(1)} %convolution_bitcast_fusion.1, pred[256,256]{1,0:T(8,128)(4,1)S(1)} %convert_compare_fusion, f32[4,256,12,64]{1,0,3,2:T(4,128)S(1)} %copy-done.6, ...), kind=kOutput, calls=%fused_computation.59 | convolution fusion | flops 2427715584 | bytes 10698752 | tf_op jit(solution)/shard_map/jvp(ctsh,cshp->cthp)/dot_general | solution.py:47
  170.9 3.7 copy.94
  174.6 8.9 %multiply_reduce_fusion.10 = (f32[1024]{0:T(1024)}, f32[1024,768]{1,0:T(8,128)}, f32[1024,768]{1,0:T(8,128)}) fusion(f32[1024]{0:T(1024)S(1)} %convert_element_type.114, f32[1024,768]{1,0:T(8,128)} %copy.94, f32[1024,768]{1,0:T(8,128)} %get-tuple-element.356, f32[768]{0:T(1024)} %mul.780, bf16[1024,1536]{1,0:T(8,128)(2,1)S(1)} %copy-done.1, ...), kind=kOutput, calls=%fused_computation.76 | convolution fusion | flops 2426928128 | bytes 18099200 | tf_op jit(solution)/shard_map/dot_general | solution.py:132
  183.5 12.5 %psum.105 = f32[1024]{0:T(1024)S(1)} all-reduce(f32[1024]{0:T(1024)} %get-tuple-element.353), channel_id=1, replica_groups=mesh['fsdp'=8,'tp'=4] {'tp'}, use_global_device_ids=true, to_apply=%region_4.5 | all-reduce | flops 1024 | bytes 8192 | tf_op jit(solution)/shard_map/psum | solution.py:180
  196.7 37.8 %all-gather.15.cloned.1.call-done = bf16[1024,1536]{1,0:T(8,128)(2,1)} async-done(((bf16[256,1536]{1,0:T(8,128)(2,1)}), bf16[1024,1536]{1,0:T(8,128)(2,1)}) %all-gather.15.cloned.1.call-update) | async-done | bytes 3145744 | tf_op jit(solution)/shard_map/all_gather | solution.py:189
  234.5 8.7 %multiply_reduce_fusion = (f32[768]{0:T(1024)}, f32[1024]{0:T(1024)}, f32[1024,768]{1,0:T(8,128)}) fusion(f32[1024,768]{1,0:T(8,128)} %get-tuple-element.354, f32[1024]{0:T(1024)} %get-tuple-element.382, f32[768]{0:T(1024)} %param.38, bf16[1024,1536]{1,0:T(8,128)(2,1)} %all-gather.15.cloned.1.call-done, bf16[768,1536]{0,1:T(8,128)(2,1)} %all-gather.13.cloned.1.call-done), kind=kOutput, calls=%fused_computation.60 | convolution fusion | flops 2420635904 | bytes 11810816 | tf_op jit(solution)/shard_map/td,cd->tc/dot_general | solution.py:190
  243.2 10.2 %psum.106 = f32[1024]{0:T(1024)} all-reduce(f32[1024]{0:T(1024)} %get-tuple-element.284), channel_id=1, replica_groups=mesh['fsdp'=8,'tp'=4] {'tp'}, use_global_device_ids=true, to_apply=%region_7.8 | all-reduce | flops 1024 | bytes 8192 | tf_op jit(solution)/shard_map/psum | solution.py:195
  254.1 8.4 %multiply_reduce_fusion.1 = (f32[768]{0:T(1024)}, f32[1024,768]{1,0:T(8,128)}, bf16[1024,768]{1,0:T(8,128)(2,1)}) fusion(f32[1024,768]{1,0:T(8,128)S(1)} %copy-done.5, f32[1024,768]{1,0:T(8,128)} %get-tuple-element.395, f32[1024]{0:T(1024)S(1)} %convert_element_type.114, f32[1024]{0:T(1024)S(1)} %broadcast_multiply_fusion.1, ...), kind=kLoop, calls=%fused_computation.61 | loop fusion | flops 21232896 | bytes 20472832 | tf_op jit(solution)/shard_map/transpose(jvp())/reduce_sum | solution.py:95
  262.4 3.6 copy.95
  266.0 3.4 reshape.262
  269.5 7.5 fusion.69
  277.0 4.3 fusion.41
  283.3 25.8 %while.37 = (s32[]{:T(128)}, f32[12,64,128]{2,1,0:T(8,128)S(1)}, f32[4,12]{1,0:T(4,128)}, f32[4,12,64,128]{3,2,1,0:T(8,128)}, f32[4,12,64,128]{3,2,1,0:T(8,128)}...) while((s32[]{:T(128)}, f32[12,64,128]{2,1,0:T(8,128)S(1)}, ...), condition=%wide.region_10.11_spmd.clone, body=%wide.region_8.10_spmd.clone.sunk | while | flops 688120 | bytes 2359756 | solution.py:62
  309.1 8.6 %fusion.70 = f32[4,256,128]{2,1,0:T(8,128)} fusion(f32[4,12,64,128]{3,2,1,0:T(8,128)} %get-tuple-element.224, f32[4,256,12,64]{1,0,3,2:T(4,128)} %reshape.258, f32[4,256,12]{1,2,0:T(8,128)} %copy-done.24, f32[4,256,12]{1,2,0:T(8,128)} %copy-done.36), kind=kOutput, calls=%fused_computation.127 | convolution fusion | flops 1209532416 | bytes 5341184 | tf_op jit(solution)/shard_map/transpose(jvp(cshp,csn->chpn))/dot_general | solution.py:51
  317.8 4.4 fusion.125
  322.2 18.7 %fusion.14 = (f32[4,256,12]{1,2,0:T(8,128)}, f32[4,256,12]{1,2,0:T(8,128)}, f32[4,256,256]{2,1,0:T(8,128)}) fusion(f32[4,256,256]{2,1,0:T(8,128)S(1)} %copy-done.32, f32[4,256,12]{1,2,0:T(8,128)S(1)} %copy-done.35, pred[256,256]{1,0:T(8,128)(4,1)S(1)} %copy-done.54, f32[4,256,12,64]{1,0,3,2:T(4,128)S(1)} %copy-done.7, f32[4,256,12]{1,2,0:T(8,128)S(1)} %copy-done.37, ...), kind=kOutput, calls=%fused_computation.25 | convolution fusion | flops 2444730368 | bytes 8650752 | tf_op jit(solution)/shard_map/transpose(jvp(ctsh,cshp->cthp))/dot_general | solution.py:47
  344.4 3.4 convolution_add_fusion
  347.8 14.3 %multiply_reduce_fusion.6 = (f32[4,256,12]{1,2,0:T(8,128)S(1)}, f32[4,256,12]{1,2,0:T(8,128)}, f32[4,256,12,64]{1,3,2,0:T(8,128)}) fusion(f32[4,256,12,64]{1,3,2,0:T(8,128)} %fusion.125, f32[4,256,12,64]{1,0,3,2:T(4,128)S(1)} %copy-done.8, f32[4,256,12]{1,2,0:T(8,128)S(1)} %copy-done.37, f32[4,256,256]{2,1,0:T(8,128)S(1)} %copy-done.33, ...), kind=kOutput, calls=%fused_computation.66 | convolution fusion | flops 2431623168 | bytes 13942784 | tf_op jit(solution)/shard_map/transpose(jvp(ctsh,cshp->cthp))/dot_general | solution.py:47
  370.0 2.9 multiply_reduce_fusion.7
  375.2 27.8 %reduce-scatter.18.cloned.1.call-done = bf16[192,256]{1,0:T(8,128)(2,1)} async-done(((bf16[1536,256]{1,0:T(8,128)(2,1)}), bf16[192,256]{1,0:T(8,128)(2,1)}) %reduce-scatter.18.cloned.1.call-update) | async-done | bytes 98320 | tf_op jit(solution)/shard_map/reduce_scatter | solution.py:230
  403.5 7.3 convolution_convert_fusion.1
  410.9 5.4 convolution_convert_fusion.3
  416.4 4.0 copy.98
  422.8 3.6 copy.99
  426.4 10.0 %multiply_reduce_fusion.5 = (f32[768]{0:T(1024)S(1)}, f32[768]{0:T(1024)S(1)}, f32[768]{0:T(1024)S(1)}, f32[768]{0:T(1024)S(1)}, f32[768]{0:T(1024)S(1)}, /*index=5*/f32[1024,768]{1,0:T(8,128)S(1)}) fusion(f32[1024,768]{1,0:T(8,128)} %copy-done.14, f32[1024]{0:T(1024)S(1)} %get-tuple-element.384, f32[1024]{0:T(1024)S(1)} %get-tuple-element.383, ...), kind=kLoop, calls=%fused_computation.65 | loop fusion | flops 18870528 | bytes 15763456 | tf_op jit(solution)/shard_map/transpose(jvp())/reduce_sum | solution.py:28
  439.8 4.0 convolution_convert_fusion.2
  456.5 5.9 convolution_convert_fusion
  464.9 12.5 %all-reduce.26.cloned.1.call-done = bf16[192,256]{1,0:T(8,128)(2,1)} async-done(((bf16[192,256]{1,0:T(8,128)(2,1)}), bf16[192,256]{1,0:T(8,128)(2,1)}) %all-reduce.26.cloned.1.call-update) | async-done | bytes 98320 | tf_op jit(solution)/shard_map/psum | solution.py:261
  479.0 43.9 %reduce-scatter.20.cloned.1.call-done = bf16[768,192]{0,1:T(8,128)(2,1)} async-done(((bf16[768,1536]{0,1:T(8,128)(2,1)}), bf16[768,192]{0,1:T(8,128)(2,1)}) %reduce-scatter.20.cloned.1.call-update) | async-done | bytes 294928 | tf_op jit(solution)/shard_map/reduce_scatter | solution.py:236
  524.7 43.8 %reduce-scatter.14.cloned.1.call-done = bf16[192,768]{1,0:T(8,128)(2,1)} async-done(((bf16[1536,768]{1,0:T(8,128)(2,1)}), bf16[192,768]{1,0:T(8,128)(2,1)}) %reduce-scatter.14.cloned.1.call-update) | async-done | bytes 294928 | tf_op jit(solution)/shard_map/reduce_scatter | solution.py:224
  570.2 43.9 %reduce-scatter.16.cloned.1.call-done = bf16[192,768]{1,0:T(8,128)(2,1)} async-done(((bf16[1536,768]{1,0:T(8,128)(2,1)}), bf16[192,768]{1,0:T(8,128)(2,1)}) %reduce-scatter.16.cloned.1.call-update) | async-done | bytes 294928 | tf_op jit(solution)/shard_map/reduce_scatter | solution.py:227
  616.0 60.8 %reduce-scatter.12.cloned.1.call-done = bf16[256,1536]{1,0:T(8,128)(2,1)} async-done(((bf16[1024,1536]{1,0:T(8,128)(2,1)}), bf16[256,1536]{1,0:T(8,128)(2,1)}) %reduce-scatter.12.cloned.1.call-update) | async-done | bytes 786448 | tf_op jit(solution)/shard_map/reduce_scatter | solution.py:212
  678.4 25.5 %all-reduce.22 = (bf16[1536]{0:T(1024)(128)(2,1)S(1)}, f32[4,768]{1,0:T(4,128)}, f32[768]{0:T(1024)}, bf16[4,256]{1,0:T(4,128)(2,1)S(1)}, bf16[256]{0:T(256)(128...) all-reduce(f32[1536]{0:T(1024)S(1)} %get-tuple-element.296, ...), channel_id=1, replica_groups=mesh['fsdp'=8,'tp'=4] {'fsdp'}, use_global_device_ids=true, to_apply=%region_21.22 | all-reduce | flops 7460 | bytes 54048 | tf_op jit(solution)/shard_map/psum | solution.py:246
  703.8 11.9 %all-reduce.23 = (bf16[1536]{0:T(1024)(128)(2,1)S(1)}, bf16[4,256]{1,0:T(4,128)(2,1)S(1)}, bf16[256]{0:T(256)(128)(2,1)S(1)}) all-reduce(bf16[1536]{0:T(1024)(128)(2,1)S(1)} %get-tuple-element.335, bf16[4,256]{1,0:T(4,128)(2,1)S(1)} %get-tuple-element.338, ...), channel_id=1, replica_groups=mesh['fsdp'=8,'tp'=4] {'tp'}, use_global_device_ids=true, to_apply=%region_22.23 | all-reduce | flops 2816 | bytes 11264 | tf_op jit(solution)/shard_map/psum | solution.py:264
  717.5 22.3 %reduce-scatter.10.cloned.1.call-done = bf16[256,1536]{1,0:T(8,128)(2,1)} async-done(((bf16[1024,1536]{1,0:T(8,128)(2,1)}), bf16[256,1536]{1,0:T(8,128)(2,1)}) %reduce-scatter.10.cloned.1.call-update) | async-done | bytes 786448 | tf_op jit(solution)/shard_map/reduce_scatter | solution.py:183
  739.8 3.2 fusion.51
  (355 shorter events, 109.0 us)
Async XLA Ops:
  7.3 19.6 %copy-start.48 = (bf16[192,256]{1,0:T(8,128)(2,1)S(1)}, bf16[192,256]{1,0:T(8,128)(2,1)}, u32[]{:S(2)}) copy-start(bf16[192,256]{1,0:T(8,128)(2,1)} %param.29) | copy-start | bytes 294916
  7.3 71.2 %copy-start.94 = (f32[12]{0:T(128)S(1)}, f32[12]{0:T(128)}, u32[]{:S(2)}) copy-start(f32[12]{0:T(128)} %param.36) | copy-start | bytes 148
  7.3 71.2 %all-gather.7.cloned.1.call-start = ((), (), s32[]{:S(2)}) async-start(), calls=%async_computation.7 | async-start | bytes 3932160 | tf_op jit(solution)/shard_map/all_gather | solution.py:131
  12.1 95.8 %all-gather.9.cloned.1.call-start = ((), (), s32[]{:S(2)}) async-start(), calls=%async_computation.8 | async-start | bytes 2654208 | tf_op jit(solution)/shard_map/all_gather | solution.py:123
  12.9 161.7 %all-gather.11.cloned.1.call-start = ((), (), s32[]{:S(2)}) async-start(), calls=%async_computation.9 | async-start | bytes 2654208 | tf_op jit(solution)/shard_map/all_gather | solution.py:122
  13.6 183.0 %all-gather.13.cloned.1.call-start = ((), (), s32[]{:S(2)}) async-start(), calls=%async_computation.10 | async-start | bytes 2654208 | tf_op jit(solution)/shard_map/all_gather | solution.py:126
  14.2 220.3 %all-gather.15.cloned.1.call-start = ((), (), s32[]{:S(2)}) async-start(), calls=%async_computation.12 | async-start | bytes 3932160 | tf_op jit(solution)/shard_map/all_gather | solution.py:189
  14.8 388.2 %reduce-scatter.18.cloned.1.call-start = ((), (), s32[]{:S(2)}) async-start(), calls=%async_computation.16 | async-start | bytes 884736 | tf_op jit(solution)/shard_map/reduce_scatter | solution.py:230
  14.9 137.4 %copy-start.53 = (pred[256,256]{1,0:T(8,128)(4,1)}, pred[256,256]{1,0:T(8,128)(4,1)S(1)}, u32[]{:S(2)}) copy-start(pred[256,256]{1,0:T(8,128)(4,1)S(1)} %convert_compare_fusion) | copy-start | bytes 196612
  15.0 67.0 %copy-start.92 = (f32[12]{0:T(128)}, f32[12]{0:T(128)S(1)}, u32[]{:S(2)}) copy-start(f32[12]{0:T(128)S(1)} %exponential_negate_fusion) | copy-start | bytes 148
  15.1 70.5 %copy-start.71 = (f32[1,256]{1,0:T(1,128)}, f32[1,256]{1,0:T(1,128)S(1)}, u32[]{:S(2)}) copy-start(f32[1,256]{1,0:T(1,128)S(1)} %get-tuple-element.387) | copy-start | bytes 3076
  15.1 70.5 %copy-start.73 = (f32[1,256]{1,0:T(1,128)}, f32[1,256]{1,0:T(1,128)S(1)}, u32[]{:S(2)}) copy-start(f32[1,256]{1,0:T(1,128)S(1)} %get-tuple-element.388) | copy-start | bytes 3076
  15.1 70.5 %copy-start.75 = (f32[1,256]{1,0:T(1,128)}, f32[1,256]{1,0:T(1,128)S(1)}, u32[]{:S(2)}) copy-start(f32[1,256]{1,0:T(1,128)S(1)} %get-tuple-element.389) | copy-start | bytes 3076
  15.1 70.5 %copy-start.77 = (f32[1,256]{1,0:T(1,128)}, f32[1,256]{1,0:T(1,128)S(1)}, u32[]{:S(2)}) copy-start(f32[1,256]{1,0:T(1,128)S(1)} %get-tuple-element.390) | copy-start | bytes 3076
  15.9 97.2 %copy-start.43 = (f32[1024]{0:T(1024)}, f32[1024]{0:T(1024)S(1)}, u32[]{:S(2)}) copy-start(f32[1024]{0:T(1024)S(1)} %get-tuple-element.386) | copy-start | bytes 12292
  15.9 97.2 %copy-start.56 = (f32[768]{0:T(1024)}, f32[768]{0:T(1024)S(1)}, u32[]{:S(2)}) copy-start(f32[768]{0:T(1024)S(1)} %get-tuple-element.299) | copy-start | bytes 9220
  15.9 97.2 %copy-start.58 = (f32[768]{0:T(1024)}, f32[768]{0:T(1024)S(1)}, u32[]{:S(2)}) copy-start(f32[768]{0:T(1024)S(1)} %get-tuple-element.300) | copy-start | bytes 9220
  16.0 97.2 %copy-start.60 = (f32[768]{0:T(1024)}, f32[768]{0:T(1024)S(1)}, u32[]{:S(2)}) copy-start(f32[768]{0:T(1024)S(1)} %get-tuple-element.301) | copy-start | bytes 9220
  16.0 97.2 %copy-start.62 = (f32[768]{0:T(1024)}, f32[768]{0:T(1024)S(1)}, u32[]{:S(2)}) copy-start(f32[768]{0:T(1024)S(1)} %get-tuple-element.302) | copy-start | bytes 9220
  26.9 55.0 %copy-start.40 = (bf16[1536,12]{0,1:T(8,128)(2,1)}, bf16[1536,12]{0,1:T(8,128)(2,1)S(1)}, u32[]{:S(2)}) copy-start(bf16[1536,12]{0,1:T(8,128)(2,1)S(1)} %reshape.277) | copy-start | bytes 110596
  37.2 48.3 %copy-start.23 = (bf16[1536,256]{1,0:T(8,128)(2,1)}, bf16[1536,256]{1,0:T(8,128)(2,1)S(1)}, u32[]{:S(2)}) copy-start(bf16[1536,256]{1,0:T(8,128)(2,1)S(1)} %all_gather.24) | copy-start | bytes 2359300
  82.0 70.4 %copy-start.36 = (f32[4,256,12]{1,2,0:T(8,128)}, f32[4,256,12]{1,2,0:T(8,128)S(1)}, u32[]{:S(2)}) copy-start(f32[4,256,12]{1,2,0:T(8,128)S(1)} %copy.90) | copy-start | bytes 147460
  82.3 70.1 %copy-start.34 = (f32[4,256,12]{1,2,0:T(8,128)}, f32[4,256,12]{1,2,0:T(8,128)S(1)}, u32[]{:S(2)}) copy-start(f32[4,256,12]{1,2,0:T(8,128)S(1)} %convolution_bitcast_fusion.1) | copy-start | bytes 147460
  82.6 45.9 %copy-start.24 = (f32[4,256,12]{1,2,0:T(8,128)}, f32[4,256,12]{1,2,0:T(8,128)S(1)}, u32[]{:S(2)}) copy-start(f32[4,256,12]{1,2,0:T(8,128)S(1)} %get-tuple-element.380) | copy-start | bytes 147460
  82.6 69.8 %copy-start.38 = (f32[4,256,12]{1,2,0:T(8,128)}, f32[4,256,12]{1,2,0:T(8,128)S(1)}, u32[]{:S(2)}) copy-start(f32[4,256,12]{1,2,0:T(8,128)S(1)} %get-tuple-element.379) | copy-start | bytes 147460
  87.6 40.9 %copy-start.12 = (f32[1024,128]{1,0:T(8,128)}, f32[1024,128]{1,0:T(8,128)S(1)}, u32[]{:S(2)}) copy-start(f32[1024,128]{1,0:T(8,128)S(1)} %get-tuple-element.373) | copy-start | bytes 1572868
  87.6 62.1 %copy-start.10 = (f32[1024,128]{1,0:T(8,128)}, f32[1024,128]{1,0:T(8,128)S(1)}, u32[]{:S(2)}) copy-start(f32[1024,128]{1,0:T(8,128)S(1)} %get-tuple-element.374) | copy-start | bytes 1572868
  87.6 25.6 %copy-start.81 = (f32[768]{0:T(1024)S(1)}, f32[768]{0:T(1024)}, u32[]{:S(2)}) copy-start(f32[768]{0:T(1024)} %param.32) | copy-start | bytes 9220
  149.6 16.8 %copy-start = (f32[4,12,64,128]{3,2,1,0:T(8,128)}, f32[4,12,64,128]{3,2,1,0:T(8,128)S(1)}, u32[]{:S(2)}) copy-start(f32[4,12,64,128]{3,2,1,0:T(8,128)S(1)} %get-tuple-element.542) | copy-start | bytes 4718596
  234.5 19.6 %copy-start.5 = (f32[1024,768]{1,0:T(8,128)S(1)}, f32[1024,768]{1,0:T(8,128)}, u32[]{:S(2)}) copy-start(f32[1024,768]{1,0:T(8,128)} %get-tuple-element.356) | copy-start | bytes 9437188
  322.2 18.7 %copy-start.65 = (f32[4,12]{1,0:T(4,128)S(1)}, f32[4,12]{1,0:T(4,128)}, u32[]{:S(2)}) copy-start(f32[4,12]{1,0:T(4,128)} %copy-done.64) | copy-start | bytes 580
  322.2 18.7 %copy-start.80 = (f32[4,12]{1,0:T(4,128)S(1)}, f32[4,12]{1,0:T(4,128)}, u32[]{:S(2)}) copy-start(f32[4,12]{1,0:T(4,128)} %get-tuple-element.225) | copy-start | bytes 580
  369.0 94.4 %reduce-scatter.22.cloned.1.call-start = ((), (), s32[]{:S(2)}) async-start(), calls=%async_computation.19 | async-start | bytes 442368
  373.3 30.1 %copy-start.66 = (f32[1024]{0:T(1024)S(1)}, f32[1024]{0:T(1024)}, u32[]{:S(2)}) copy-start(f32[1024]{0:T(1024)} %get-tuple-element.382) | copy-start | bytes 12292
  373.4 30.1 %copy-start.82 = (f32[768]{0:T(1024)S(1)}, f32[768]{0:T(1024)}, u32[]{:S(2)}) copy-start(f32[768]{0:T(1024)} %param.38) | copy-start | bytes 9220
  375.2 102.2 %all-reduce.26.cloned.1.call-start = ((), (), s32[]{:S(2)}) async-start(), calls=%async_computation.17 | async-start | bytes 196608 | tf_op jit(solution)/shard_map/psum | solution.py:261
  403.0 119.8 %reduce-scatter.20.cloned.1.call-start = ((), (), s32[]{:S(2)}) async-start(), calls=%async_computation.18 | async-start | bytes 2654208 | tf_op jit(solution)/shard_map/reduce_scatter | solution.py:236
  410.8 157.6 %reduce-scatter.14.cloned.1.call-start = ((), (), s32[]{:S(2)}) async-start(), calls=%async_computation.14 | async-start | bytes 2654208 | tf_op jit(solution)/shard_map/reduce_scatter | solution.py:224
  416.3 197.8 %reduce-scatter.16.cloned.1.call-start = ((), (), s32[]{:S(2)}) async-start(), calls=%async_computation.15 | async-start | bytes 2654208 | tf_op jit(solution)/shard_map/reduce_scatter | solution.py:227
  443.9 232.9 %reduce-scatter.12.cloned.1.call-start = ((), (), s32[]{:S(2)}) async-start(), calls=%async_computation.13 | async-start | bytes 3932160 | tf_op jit(solution)/shard_map/reduce_scatter | solution.py:212
  454.6 285.2 %reduce-scatter.10.cloned.1.call-start = ((), (), s32[]{:S(2)}) async-start(), calls=%async_computation.11 | async-start | bytes 3932160 | tf_op jit(solution)/shard_map/reduce_scatter | solution.py:183
  462.4 214.3 %copy-start.16 = (bf16[256,1536]{1,0:T(8,128)(2,1)S(1)}, bf16[256,1536]{1,0:T(8,128)(2,1)}, u32[]{:S(2)}) copy-start(bf16[256,1536]{1,0:T(8,128)(2,1)} %param.22) | copy-start | bytes 2359300
  462.4 214.3 %copy-start.49 = (f32[1536]{0:T(1024)S(1)}, f32[1536]{0:T(1024)}, u32[]{:S(2)}) copy-start(f32[1536]{0:T(1024)} %param.26) | copy-start | bytes 18436
  462.5 214.3 %copy-start.69 = (f32[256]{0:T(256)S(1)}, f32[256]{0:T(256)}, u32[]{:S(2)}) copy-start(f32[256]{0:T(256)} %copy-done.68) | copy-start | bytes 3076
  462.5 215.9 %copy-start.84 = (f32[768]{0:T(1024)S(1)}, f32[768]{0:T(1024)}, u32[]{:S(2)}) copy-start(f32[768]{0:T(1024)} %get-tuple-element.283) | copy-start | bytes 9220
  462.5 215.8 %copy-start.87 = (f32[256]{0:T(256)S(1)}, f32[256]{0:T(256)}, u32[]{:S(2)}) copy-start(f32[256]{0:T(256)} %get-tuple-element.298) | copy-start | bytes 3076
  462.5 277.3 %copy-start.21 = (bf16[256,1536]{1,0:T(8,128)(2,1)S(1)}, bf16[256,1536]{1,0:T(8,128)(2,1)}, u32[]{:S(2)}) copy-start(bf16[256,1536]{1,0:T(8,128)(2,1)} %param.23) | copy-start | bytes 2359300
  462.5 277.3 %copy-start.83 = (f32[256]{0:T(256)S(1)}, f32[256]{0:T(256)}, u32[]{:S(2)}) copy-start(f32[256]{0:T(256)} %get-tuple-element.391) | copy-start | bytes 3076
  (68 other events, 346.1 us)
Sparse Core Ops, SparseCore 0:
  12.3 66.1 all-gather.6
  80.3 27.5 all-gather.8
  109.8 28.8 all-gather.10
  140.4 28.9 all-gather.12
  170.8 63.6 all-gather.14
  369.1 33.7 reduce-scatter.17
  406.6 33.9 reduce-scatter.21
  442.9 34.4 all-reduce.25
  480.7 42.0 reduce-scatter.19
  526.0 42.3 reduce-scatter.13
  571.8 42.3 reduce-scatter.15
  616.3 60.3 reduce-scatter.11
  679.0 60.7 reduce-scatter.9
where the time goes:
time: 761 us; the launch traced here: 750 us
  waiting for transfers between devices  357 us (47%)
  matrix products  154 us (20%)
  blocking collectives  81.3 us (11%)
  other arithmetic  78.7 us (10%)
  local copies, waits for them, and re-layouts  61.8 us (8%)
  between operations  15.6 us (2%)
    reduce_scatter x1, waiting for transfers between devices, shards(): lax.psum_scatter((partial_term(grad_z, whole_z) + partial_term(grad_x, wh...  60.8 us
    dot_general x3, matrix products, state_scan(): jnp.einsum('ctsh,cshp->cthp', weights * intersection[..., None], scaled_x...  47.1 us
    reduce_scatter x1, waiting for transfers between devices, shards(): lax.psum_scatter(weight_x.astype(jnp.bfloat16), 'fsdp', scatter_dimension...  43.9 us
    reduce_scatter x1, waiting for transfers between devices, shards(): lax.psum_scatter(grad_out_rows.astype(jnp.bfloat16), 'fsdp', scatter_dime...  43.9 us
    reduce_scatter x1, waiting for transfers between devices, shards(): lax.psum_scatter(weight_z.astype(jnp.bfloat16), 'fsdp', scatter_dimension...  43.8 us
    all_gather x1, waiting for transfers between devices, shards(): normed_all = lax.all_gather(normed, 'tp', axis=0, tiled=True)  41.2 us
    all_gather x1, waiting for transfers between devices, shards(): cot_all = lax.all_gather(cotangent, 'tp', axis=0, tiled=True)  37.8 us
    reduce_scatter x1, waiting for transfers between devices, shards(): lax.psum_scatter(weight_bc.astype(jnp.bfloat16), 'fsdp', scatter_dimensio...  27.8 us
  transfers between devices with their start and end apart: 13, of which 10 were waited for; matrix products, arithmetic and copies ran while one was open for 21% of the time, Pallas kernels for 0%

commit v1 on v0

--- a/solution.py
+++ b/solution.py
@@ -9,6 +9,12 @@
 INNER = 3072
 EPSILON = 1e-05
 PRECISE = lax.Precision.HIGHEST
+
+
+def laid_out(pieces, dim):
+    dims = list(pieces.shape[1:])
+    dims[dim] *= pieces.shape[0]
+    return jnp.moveaxis(pieces, 0, dim).reshape(dims)
 
 
 def causal_conv(signal, kernel, offset_bias, openings):
@@ -128,7 +134,19 @@
     resid = tokens.astype(jnp.float32)
     rstd = lax.rsqrt(jnp.mean(resid * resid, axis=1, keepdims=True) + EPSILON)
     normed = (resid * rstd * norm_gain[None, :]).astype(jnp.bfloat16)
-    normed_all = lax.all_gather(normed, "tp", axis=0, tiled=True)
+    devices = lax.axis_size("tp")
+    pairs = [(i, (i + 1) % devices) for i in range(devices)]
+    back = [(b, a) for a, b in pairs]
+    lower_2, upper = ([], [])
+    for step in range(devices - 1):
+        if step % 2 == 0:
+            lower_2.append(lax.ppermute(lower_2[-1] if lower_2 else normed, "tp", pairs))
+        else:
+            upper.append(lax.ppermute(upper[-1] if upper else normed, "tp", back))
+    blocks = jnp.stack([*lower_2[::-1], normed, *upper])
+    shift = lax.axis_index("tp") - len(lower_2)
+    blocks = blocks[(jnp.arange(devices) - shift) % devices]
+    normed_all = laid_out(blocks, 0)
     pre_z = jnp.dot(normed_all, whole_z, preferred_element_type=jnp.float32)
     pre_x = jnp.dot(normed_all, whole_x, preferred_element_type=jnp.float32)
     pre_bc = jnp.dot(normed_all, whole_bc, preferred_element_type=jnp.float32)

time: 761 us -> 720 us (0.946)
  waiting for transfers between devices: 357 us -> 280 us
  other arithmetic: 78.7 us -> 99.3 us
  local copies, waits for them, and re-layouts: 61.8 us -> 76.6 us
    all_gather x1 -> x0, waiting for transfers between devices: 41.2 us -> none  [shards(): normed_all = lax.all_gather(normed, 'tp', axis=0, tiled=True)]
    all_gather x1, waiting for transfers between devices: 37.8 us -> 0.01 us  [shards(): cot_all = lax.all_gather(cotangent, 'tp', axis=0, tiled=True)]
    ppermute x0 -> x3, waiting for transfers between devices: none -> 24.3 us  [the longest x2 24.3 us: shards(): lax.ppermute(lower_2[-1] if lower_2 else normed, 'tp', pairs)]
    all_gather x1, waiting for transfers between devices: 20.3 us -> 0.01 us  [shards(): lax.all_gather(proj_x, 'fsdp', axis=0, tiled=True)]
    dynamic_update_slice x12, other arithmetic: 8.3 us -> 17.3 us  [state_scan(): lax.scan(advance, initial, (openings, carry_decay, block_states))]
  transfers between devices with their start and end apart: 13 -> 15, of which waited for: 10 -> 9; matrix products, arithmetic and copies ran while one was open for 21% -> 28% of each run, Pallas kernels for 0% -> 0%
where the time goes in v1:
time: 720 us; the launch traced here: 715 us
  waiting for transfers between devices  280 us (39%)
  matrix products  155 us (22%)
  other arithmetic  99.3 us (14%)
  blocking collectives  80 us (11%)
  local copies, waits for them, and re-layouts  76.6 us (11%)
  between operations  15.7 us (2%)
  starting transfers between devices  7.55 us (1%)
    reduce_scatter x1, waiting for transfers between devices, shards(): lax.psum_scatter((partial_term(grad_z, whole_z) + partial_term(grad_x, wh...  60.9 us
    dot_general x3, matrix products, state_scan(): jnp.einsum('ctsh,cshp->cthp', weights * intersection[..., None], scaled_x...  47.9 us
    reduce_scatter x1, waiting for transfers between devices, shards(): lax.psum_scatter(weight_z.astype(jnp.bfloat16), 'fsdp', scatter_dimension...  43.9 us
    reduce_scatter x1, waiting for transfers between devices, shards(): lax.psum_scatter(grad_out_rows.astype(jnp.bfloat16), 'fsdp', scatter_dime...  43.9 us
    reduce_scatter x1, waiting for transfers between devices, shards(): lax.psum_scatter(weight_x.astype(jnp.bfloat16), 'fsdp', scatter_dimension...  43.8 us
    reduce_scatter x1, waiting for transfers between devices, shards(): lax.psum_scatter(weight_bc.astype(jnp.bfloat16), 'fsdp', scatter_dimensio...  26.8 us
    psum x1, blocking collectives, shards(): lax.psum((grads[4], grads[5], grads[6], grads[7], grads[8], grads[9], gra...  25.5 us
    ppermute x2, waiting for transfers between devices, shards(): lax.ppermute(lower_2[-1] if lower_2 else normed, 'tp', pairs)  24.3 us
  transfers between devices with their start and end apart: 15, of which 9 were waited for; matrix products, arithmetic and copies ran while one was open for 28% of the time, Pallas kernels for 0%

profile of v1, /device:TPU:0, one launch (start us, length us, event | category | flops | bytes accessed | tf_op | source)
XLA Modules:
  0.0 715.1 jit_solution(13209702375002616573)
XLA Ops:
  13.7 5.1 collective-permute-start.2
  20.9 9.3 %all-gather = bf16[8,192,12]{1,2,0:T(8,128)(2,1)S(1)} all-gather(bf16[1,192,12]{1,2,0:T(8,128)(2,1)S(1)} %bitcast.226), channel_id=1, replica_groups=mesh['fsdp'=8,'tp'=4] {'fsdp'}, dimensions={0}, use_global_device_ids=true | all-gather | bytes 41472 | tf_op jit(solution)/shard_map/all_gather | solution.py:131
  31.6 13.0 %all_gather.20 = bf16[1536,256]{1,0:T(8,128)(2,1)} all-gather(bf16[192,256]{1,0:T(8,128)(2,1)S(1)} %copy-done.41), channel_id=1, replica_groups=mesh['fsdp'=8,'tp'=4] {'fsdp'}, dimensions={0}, use_global_device_ids=true | all-gather | bytes 884736 | tf_op jit(solution)/shard_map/all_gather | solution.py:130
  45.7 7.9 %collective-permute-done = bf16[256,1536]{1,0:T(8,128)(2,1)S(1)} collective-permute-done((bf16[256,1536]{1,0:T(8,128)(2,1)}, bf16[256,1536]{1,0:T(8,128)(2,1)S(1)}, u32[]{:S(2)}, u32[]{:S(2)}) %collective-permute-start) | collective-permute-done | bytes 786464 | tf_op jit(solution)/shard_map/ppermute | solution.py:143
  57.5 16.4 %collective-permute-done.1 = bf16[256,1536]{1,0:T(8,128)(2,1)S(1)} collective-permute-done((bf16[256,1536]{1,0:T(8,128)(2,1)S(1)}, bf16[256,1536]{1,0:T(8,128)(2,1)S(1)}, u32[]{:S(2)}, u32[]{:S(2)}) %collective-permute-start.1) | collective-permute-done | bytes 786464 | tf_op jit(solution)/shard_map/ppermute | solution.py:143
  75.8 2.8 gather_fusion
  93.7 4.3 fusion.122
  98.1 4.7 fusion.32
  102.8 3.6 copy.88
  106.3 5.2 reshape.311
  111.5 6.4 fusion.38
  119.3 32.4 %while.36 = (s32[]{:T(128)}, f32[12,64,128]{2,1,0:T(8,128)}, f32[4,12,64,128]{3,2,1,0:T(8,128)}, f32[4]{0:T(128)}, f32[4,12,1,1]{1,3,2,0:T(1,128)}, /*index=5*/f...) while((s32[]{:T(128)}, f32[12,64,128]{2,1,0:T(8,128)}, ...), condition=%wide.region_2.3_spmd.clone, body=%wide.region_1.2_spmd.clone.sunk | while | flops 589828 | bytes 1968436 | solution.py:68
  151.8 4.3 fusion.125
  156.2 14.3 %bitcast_add_fusion.3 = f32[4,256,12,64]{1,3,2,0:T(8,128)S(1)} fusion(f32[4,256,12,64]{1,3,2,0:T(8,128)S(1)} %fusion.125, f32[4,256,256]{2,1,0:T(8,128)S(1)} %copy-done.25, f32[4,256,12]{1,2,0:T(8,128)S(1)} %copy-done.29, pred[256,256]{1,0:T(8,128)(4,1)S(1)} %copy-done.44, f32[4,256,12,64]{1,0,3,2:T(4,128)S(1)} %copy-done.3, ...), kind=kOutput, calls=%fused_computation.61 | convolution fusion | flops 2427715584 | bytes 10698752 | tf_op jit(solution)/shard_map/jvp(ctsh,cshp->cthp)/dot_general | solution.py:53
  174.9 3.6 copy.94
  178.5 8.8 %multiply_reduce_fusion.10 = (f32[1024]{0:T(1024)}, f32[1024,768]{1,0:T(8,128)}, f32[1024,768]{1,0:T(8,128)}) fusion(f32[1024]{0:T(1024)S(1)} %convert_element_type.114, f32[1024,768]{1,0:T(8,128)} %copy.94, f32[1024,768]{1,0:T(8,128)} %get-tuple-element.356, f32[768]{0:T(1024)} %mul.780, bf16[1024,1536]{1,0:T(8,128)(2,1)S(1)} %bitcast.188, ...), kind=kOutput, calls=%fused_computation.78 | convolution fusion | flops 2426928128 | bytes 18099200 | tf_op jit(solution)/shard_map/dot_general | solution.py:150
  187.3 9.1 %psum.105 = f32[1024]{0:T(1024)} all-reduce(f32[1024]{0:T(1024)} %get-tuple-element.353), channel_id=1, replica_groups=mesh['fsdp'=8,'tp'=4] {'tp'}, use_global_device_ids=true, to_apply=%region_4.5 | all-reduce | flops 1024 | bytes 8192 | tf_op jit(solution)/shard_map/psum | solution.py:198
  197.6 8.6 %multiply_reduce_fusion = (f32[768]{0:T(1024)}, f32[1024]{0:T(1024)}, f32[1024,768]{1,0:T(8,128)}) fusion(f32[1024,768]{1,0:T(8,128)} %get-tuple-element.354, f32[1024]{0:T(1024)} %get-tuple-element.382, f32[768]{0:T(1024)} %param.38, bf16[1024,1536]{1,0:T(8,128)(2,1)} %all-gather.12.cloned.1.call-done, bf16[768,1536]{0,1:T(8,128)(2,1)} %all-gather.10.cloned.1.call-done), kind=kOutput, calls=%fused_computation.62 | convolution fusion | flops 2420635904 | bytes 11810816 | tf_op jit(solution)/shard_map/td,cd->tc/dot_general | solution.py:208
  206.2 11.2 %psum.106 = f32[1024]{0:T(1024)} all-reduce(f32[1024]{0:T(1024)} %get-tuple-element.284), channel_id=1, replica_groups=mesh['fsdp'=8,'tp'=4] {'tp'}, use_global_device_ids=true, to_apply=%region_7.8 | all-reduce | flops 1024 | bytes 8192 | tf_op jit(solution)/shard_map/psum | solution.py:213
  218.1 9.1 %multiply_reduce_fusion.1 = (f32[768]{0:T(1024)}, f32[1024,768]{1,0:T(8,128)}, bf16[1024,768]{1,0:T(8,128)(2,1)}) fusion(f32[1024,768]{1,0:T(8,128)} %get-tuple-element.356, f32[1024,768]{1,0:T(8,128)} %get-tuple-element.395, f32[1024]{0:T(1024)S(1)} %convert_element_type.114, f32[1024]{0:T(1024)S(1)} %broadcast_multiply_fusion.1, ...), kind=kLoop, calls=%fused_computation.63 | loop fusion | flops 21232896 | bytes 20472832 | tf_op jit(solution)/shard_map/transpose(jvp())/reduce_sum | solution.py:101
  227.3 3.6 copy.95
  230.8 5.1 reshape.315
  236.0 8.5 %fusion.69 = f32[4,256,128]{2,1,0:T(8,128)} fusion(f32[4,12,64,128]{3,2,1,0:T(8,128)} %get-tuple-element.542, f32[4,256,12,64]{1,0,3,2:T(4,128)} %reshape.315, f32[4,256,12]{1,2,0:T(8,128)} %get-tuple-element.379), kind=kOutput, calls=%fused_computation.128 | convolution fusion | flops 1208745984 | bytes 5292032 | tf_op jit(solution)/shard_map/transpose(jvp(ctn,chpn->cthp))/dot_general | solution.py:70
  244.5 4.3 fusion.41
  250.8 25.8 %while.37 = (s32[]{:T(128)}, f32[12,64,128]{2,1,0:T(8,128)S(1)}, f32[4,12]{1,0:T(4,128)}, f32[4,12,64,128]{3,2,1,0:T(8,128)}, f32[4,12,64,128]{3,2,1,0:T(8,128)}...) while((s32[]{:T(128)}, f32[12,64,128]{2,1,0:T(8,128)S(1)}, ...), condition=%wide.region_10.11_spmd.clone, body=%wide.region_8.10_spmd.clone.sunk | while | flops 688120 | bytes 2359756 | solution.py:68
  276.6 8.6 %fusion.70 = f32[4,256,128]{2,1,0:T(8,128)} fusion(f32[4,12,64,128]{3,2,1,0:T(8,128)} %get-tuple-element.224, f32[4,256,12,64]{1,0,3,2:T(4,128)} %reshape.311, f32[4,256,12]{1,2,0:T(8,128)} %get-tuple-element.380, f32[4,256,12]{1,2,0:T(8,128)} %copy.90), kind=kOutput, calls=%fused_computation.129 | convolution fusion | flops 1209532416 | bytes 5341184 | tf_op jit(solution)/shard_map/transpose(jvp(cshp,csn->chpn))/dot_general | solution.py:57
  285.2 4.3 fusion.127
  289.6 18.9 %fusion.14 = (f32[4,256,12]{1,2,0:T(8,128)S(1)}, f32[4,256,12]{1,2,0:T(8,128)}, f32[4,256,256]{2,1,0:T(8,128)}) fusion(f32[4,256,256]{2,1,0:T(8,128)S(1)} %copy-done.26, f32[4,256,12]{1,2,0:T(8,128)S(1)} %copy-done.30, pred[256,256]{1,0:T(8,128)(4,1)S(1)} %copy-done.45, f32[4,256,12,64]{1,0,3,2:T(4,128)S(1)} %copy-done.4, f32[4,256,12]{1,2,0:T(8,128)S(1)} %copy-done.32, ...), kind=kOutput, calls=%fused_computation.26 | convolution fusion | flops 2444730368 | bytes 8650752 | tf_op jit(solution)/shard_map/transpose(jvp(ctsh,cshp->cthp))/dot_general | solution.py:53
  311.4 3.4 convolution_add_fusion
  314.8 14.7 %multiply_reduce_fusion.6 = (f32[4,256,12]{1,2,0:T(8,128)S(1)}, f32[4,256,12]{1,2,0:T(8,128)}, f32[4,256,12,64]{1,3,2,0:T(8,128)}) fusion(f32[4,256,12,64]{1,3,2,0:T(8,128)} %fusion.127, f32[4,256,12,64]{1,0,3,2:T(4,128)} %reshape.311, f32[4,256,12]{1,2,0:T(8,128)S(1)} %copy-done.32, f32[4,256,256]{2,1,0:T(8,128)S(1)} %copy-done.27, ...), kind=kOutput, calls=%fused_computation.68 | convolution fusion | flops 2431623168 | bytes 13942784 | tf_op jit(solution)/shard_map/transpose(jvp(ctsh,cshp->cthp))/dot_general | solution.py:53
  335.2 3.8 multiply_reduce_fusion.7
  341.3 26.8 %reduce-scatter.18.cloned.1.call-done = bf16[192,256]{1,0:T(8,128)(2,1)} async-done(((bf16[1536,256]{1,0:T(8,128)(2,1)}), bf16[192,256]{1,0:T(8,128)(2,1)}) %reduce-scatter.18.cloned.1.call-update) | async-done | bytes 98320 | tf_op jit(solution)/shard_map/reduce_scatter | solution.py:248
  368.2 7.0 convolution_convert_fusion.1
  375.4 5.5 convolution_convert_fusion.3
  381.0 4.0 copy.98
  387.3 3.5 copy.99
  390.9 10.8 %multiply_reduce_fusion.5 = (f32[768]{0:T(1024)S(1)}, f32[768]{0:T(1024)S(1)}, f32[768]{0:T(1024)S(1)}, f32[768]{0:T(1024)S(1)}, f32[768]{0:T(1024)S(1)}, /*index=5*/f32[1024,768]{1,0:T(8,128)S(1)}) fusion(f32[1024,768]{1,0:T(8,128)} %copy-done.12, f32[1024]{0:T(1024)S(1)} %get-tuple-element.384, f32[1024]{0:T(1024)S(1)} %get-tuple-element.383, ...), kind=kLoop, calls=%fused_computation.67 | loop fusion | flops 18870528 | bytes 15763456 | tf_op jit(solution)/shard_map/transpose(jvp())/reduce_sum | solution.py:34
  405.1 4.0 convolution_convert_fusion.2
  421.9 5.9 convolution_convert_fusion
  430.3 12.1 %all-reduce.26.cloned.1.call-done = bf16[192,256]{1,0:T(8,128)(2,1)} async-done(((bf16[192,256]{1,0:T(8,128)(2,1)}), bf16[192,256]{1,0:T(8,128)(2,1)}) %all-reduce.26.cloned.1.call-update) | async-done | bytes 98320 | tf_op jit(solution)/shard_map/psum | solution.py:279
  443.9 43.9 %reduce-scatter.20.cloned.1.call-done = bf16[768,192]{0,1:T(8,128)(2,1)} async-done(((bf16[768,1536]{0,1:T(8,128)(2,1)}), bf16[768,192]{0,1:T(8,128)(2,1)}) %reduce-scatter.20.cloned.1.call-update) | async-done | bytes 294928 | tf_op jit(solution)/shard_map/reduce_scatter | solution.py:254
  489.6 43.9 %reduce-scatter.14.cloned.1.call-done = bf16[192,768]{1,0:T(8,128)(2,1)} async-done(((bf16[1536,768]{1,0:T(8,128)(2,1)}), bf16[192,768]{1,0:T(8,128)(2,1)}) %reduce-scatter.14.cloned.1.call-update) | async-done | bytes 294928 | tf_op jit(solution)/shard_map/reduce_scatter | solution.py:242
  535.4 43.8 %reduce-scatter.16.cloned.1.call-done = bf16[192,768]{1,0:T(8,128)(2,1)} async-done(((bf16[1536,768]{1,0:T(8,128)(2,1)}), bf16[192,768]{1,0:T(8,128)(2,1)}) %reduce-scatter.16.cloned.1.call-update) | async-done | bytes 294928 | tf_op jit(solution)/shard_map/reduce_scatter | solution.py:245
  580.9 60.9 %reduce-scatter.12.cloned.1.call-done = bf16[256,1536]{1,0:T(8,128)(2,1)} async-done(((bf16[1024,1536]{1,0:T(8,128)(2,1)}), bf16[256,1536]{1,0:T(8,128)(2,1)}) %reduce-scatter.12.cloned.1.call-update) | async-done | bytes 786448 | tf_op jit(solution)/shard_map/reduce_scatter | solution.py:230
  643.5 25.5 %all-reduce.22 = (bf16[1536]{0:T(1024)(128)(2,1)S(1)}, f32[4,768]{1,0:T(4,128)}, f32[768]{0:T(1024)}, bf16[4,256]{1,0:T(4,128)(2,1)S(1)}, bf16[256]{0:T(256)(128...) all-reduce(f32[1536]{0:T(1024)S(1)} %get-tuple-element.296, ...), channel_id=1, replica_groups=mesh['fsdp'=8,'tp'=4] {'fsdp'}, use_global_device_ids=true, to_apply=%region_21.22 | all-reduce | flops 7460 | bytes 54048 | tf_op jit(solution)/shard_map/psum | solution.py:264
  668.9 11.9 %all-reduce.23 = (bf16[1536]{0:T(1024)(128)(2,1)S(1)}, bf16[4,256]{1,0:T(4,128)(2,1)S(1)}, bf16[256]{0:T(256)(128)(2,1)S(1)}) all-reduce(bf16[1536]{0:T(1024)(128)(2,1)S(1)} %get-tuple-element.335, bf16[4,256]{1,0:T(4,128)(2,1)S(1)} %get-tuple-element.338, ...), channel_id=1, replica_groups=mesh['fsdp'=8,'tp'=4] {'tp'}, use_global_device_ids=true, to_apply=%region_22.23 | all-reduce | flops 2816 | bytes 11264 | tf_op jit(solution)/shard_map/psum | solution.py:282
  682.6 22.2 %reduce-scatter.10.cloned.1.call-done = bf16[256,1536]{1,0:T(8,128)(2,1)} async-done(((bf16[1024,1536]{1,0:T(8,128)(2,1)}), bf16[256,1536]{1,0:T(8,128)(2,1)}) %reduce-scatter.10.cloned.1.call-update) | async-done | bytes 786448 | tf_op jit(solution)/shard_map/reduce_scatter | solution.py:201
  704.8 3.2 fusion.51
  (331 shorter events, 141.3 us)
Async XLA Ops:
  7.2 49.4 %copy-start.5 = (bf16[256,1536]{1,0:T(8,128)(2,1)S(1)}, bf16[256,1536]{1,0:T(8,128)(2,1)}, u32[]{:S(2)}) copy-start(bf16[256,1536]{1,0:T(8,128)(2,1)} %param.22) | copy-start | bytes 2359300
  7.2 12.4 %copy-start.84 = (s32[4]{0:T(128)S(1)}, s32[4]{0:T(128)}, u32[]{:S(2)}) copy-start(s32[4]{0:T(128)} %param.24) | copy-start | bytes 52
  7.2 12.5 %copy-start.77 = (s32[1024]{0:T(1024)S(1)}, s32[1024]{0:T(1024)}, u32[]{:S(2)}) copy-start(s32[1024]{0:T(1024)} %param.25) | copy-start | bytes 12292
  7.2 12.9 %copy-start.81 = (f32[12]{0:T(128)S(1)}, f32[12]{0:T(128)}, u32[]{:S(2)}) copy-start(f32[12]{0:T(128)} %param.37) | copy-start | bytes 148
  7.2 13.7 %copy-start.71 = (bf16[192,12]{0,1:T(8,128)(2,1)S(1)}, bf16[192,12]{0,1:T(8,128)(2,1)}, u32[]{:S(2)}) copy-start(bf16[192,12]{0,1:T(8,128)(2,1)} %param.30) | copy-start | bytes 13828
  7.2 23.7 %copy-start.62 = (f32[4,768]{1,0:T(4,128)S(1)}, f32[4,768]{1,0:T(4,128)}, u32[]{:S(2)}) copy-start(f32[4,768]{1,0:T(4,128)} %param.31) | copy-start | bytes 36868
  7.2 24.4 %copy-start.41 = (bf16[192,256]{1,0:T(8,128)(2,1)S(1)}, bf16[192,256]{1,0:T(8,128)(2,1)}, u32[]{:S(2)}) copy-start(bf16[192,256]{1,0:T(8,128)(2,1)} %param.29) | copy-start | bytes 294916
  7.3 37.3 %copy-start.85 = (f32[12]{0:T(128)S(1)}, f32[12]{0:T(128)}, u32[]{:S(2)}) copy-start(f32[12]{0:T(128)} %param.35) | copy-start | bytes 148
  7.3 37.8 %copy-start.78 = (f32[4,256]{1,0:T(4,128)S(1)}, f32[4,256]{1,0:T(4,128)}, u32[]{:S(2)}) copy-start(f32[4,256]{1,0:T(4,128)} %param.33) | copy-start | bytes 12292
  7.3 86.4 %all-gather.6.cloned.1.call-start = ((), (), s32[]{:S(2)}) async-start(), calls=%async_computation.7 | async-start | bytes 2654208 | tf_op jit(solution)/shard_map/all_gather | solution.py:129
  8.0 170.5 %all-gather.8.cloned.1.call-start = ((), (), s32[]{:S(2)}) async-start(), calls=%async_computation.8 | async-start | bytes 2654208 | tf_op jit(solution)/shard_map/all_gather | solution.py:128
  8.8 188.8 %all-gather.10.cloned.1.call-start = ((), (), s32[]{:S(2)}) async-start(), calls=%async_computation.9 | async-start | bytes 2654208 | tf_op jit(solution)/shard_map/all_gather | solution.py:132
  9.5 188.1 %all-gather.12.cloned.1.call-start = ((), (), s32[]{:S(2)}) async-start(), calls=%async_computation.11 | async-start | bytes 3932160 | tf_op jit(solution)/shard_map/all_gather | solution.py:207
  13.7 43.8 %collective-permute-start.2 = (bf16[256,1536]{1,0:T(8,128)(2,1)}, bf16[256,1536]{1,0:T(8,128)(2,1)S(1)}, u32[]{:S(2)}, u32[]{:S(2)}) collective-permute-start(bf16[256,1536]{1,0:T(8,128)(2,1)} %fusion.54), channel_id=1, source_target_pairs={{1,0},{2,1},{3,2},{0,3},{5,4},{6,5},{7,6},{4,7},{9,8},{10,9},{11,1... | collective-permute-start | bytes 2359304 | tf_op jit(solution)/shard_map/ppermute | solution.py:145
  18.8 34.8 %collective-permute-start = (bf16[256,1536]{1,0:T(8,128)(2,1)}, bf16[256,1536]{1,0:T(8,128)(2,1)S(1)}, u32[]{:S(2)}, u32[]{:S(2)}) collective-permute-start(bf16[256,1536]{1,0:T(8,128)(2,1)} %fusion.54), channel_id=1, source_target_pairs={{0,1},{1,2},{2,3},{3,0},{4,5},{5,6},{6,7},{7,4},{8,9},{9,10},{10,1... | collective-permute-start | bytes 2359304 | tf_op jit(solution)/shard_map/ppermute | solution.py:143
  18.8 349.3 %reduce-scatter.18.cloned.1.call-start = ((), (), s32[]{:S(2)}) async-start(), calls=%async_computation.15 | async-start | bytes 884736 | tf_op jit(solution)/shard_map/reduce_scatter | solution.py:248
  53.6 20.4 %collective-permute-start.1 = (bf16[256,1536]{1,0:T(8,128)(2,1)S(1)}, bf16[256,1536]{1,0:T(8,128)(2,1)S(1)}, u32[]{:S(2)}, u32[]{:S(2)}) collective-permute-start(bf16[256,1536]{1,0:T(8,128)(2,1)S(1)} %collective-permute-done), channel_id=1, source_target_pairs={{0,1},{1,2},{2,3},{3,0},{4,5},{5,6},{6,7},{7,4},{8,9},{9,10},{10,1... | collective-permute-start | bytes 2359304 | tf_op jit(solution)/shard_map/ppermute | solution.py:143
  156.1 14.3 %copy-start.13 = (f32[4,256,12,64]{1,3,2,0:T(8,128)}, f32[4,256,12,64]{1,3,2,0:T(8,128)S(1)}, u32[]{:S(2)}) copy-start(f32[4,256,12,64]{1,3,2,0:T(8,128)S(1)} %fusion.125) | copy-start | bytes 9437188
  236.0 8.5 %copy-start = (f32[4,256,12,64]{1,0,3,2:T(4,128)S(1)}, f32[4,256,12,64]{1,0,3,2:T(4,128)}, u32[]{:S(2)}) copy-start(f32[4,256,12,64]{1,0,3,2:T(4,128)} %reshape.315) | copy-start | bytes 9437188
  236.0 8.5 %copy-start.9 = (f32[1024,128]{1,0:T(8,128)S(1)}, f32[1024,128]{1,0:T(8,128)}, u32[]{:S(2)}) copy-start(f32[1024,128]{1,0:T(8,128)} %copy-done.8) | copy-start | bytes 1572868
  236.0 8.5 %copy-start.34 = (f32[4,256,12]{1,2,0:T(8,128)S(1)}, f32[4,256,12]{1,2,0:T(8,128)}, u32[]{:S(2)}) copy-start(f32[4,256,12]{1,2,0:T(8,128)} %get-tuple-element.379) | copy-start | bytes 147460
  276.6 8.6 %copy-start.7 = (f32[4,12,64,128]{3,2,1,0:T(8,128)S(1)}, f32[4,12,64,128]{3,2,1,0:T(8,128)}, u32[]{:S(2)}) copy-start(f32[4,12,64,128]{3,2,1,0:T(8,128)} %get-tuple-element.224) | copy-start | bytes 4718596
  276.6 8.6 %copy-start.11 = (f32[1024,128]{1,0:T(8,128)S(1)}, f32[1024,128]{1,0:T(8,128)}, u32[]{:S(2)}) copy-start(f32[1024,128]{1,0:T(8,128)} %copy-done.10) | copy-start | bytes 1572868
  276.6 13.0 %copy-start.4 = (f32[4,256,12,64]{1,0,3,2:T(4,128)S(1)}, f32[4,256,12,64]{1,0,3,2:T(4,128)}, u32[]{:S(2)}) copy-start(f32[4,256,12,64]{1,0,3,2:T(4,128)} %reshape.311) | copy-start | bytes 9437188
  289.6 18.9 %copy-start.56 = (f32[4,12]{1,0:T(4,128)S(1)}, f32[4,12]{1,0:T(4,128)}, u32[]{:S(2)}) copy-start(f32[4,12]{1,0:T(4,128)} %copy-done.55) | copy-start | bytes 580
  289.6 18.9 %copy-start.72 = (f32[4,12]{1,0:T(4,128)S(1)}, f32[4,12]{1,0:T(4,128)}, u32[]{:S(2)}) copy-start(f32[4,12]{1,0:T(4,128)} %get-tuple-element.225) | copy-start | bytes 580
  314.8 14.8 %copy-start.15 = (f32[1024,256]{1,0:T(8,128)S(1)}, f32[1024,256]{1,0:T(8,128)}, u32[]{:S(2)}) copy-start(f32[1024,256]{1,0:T(8,128)} %copy-done.14) | copy-start | bytes 3145732
  314.8 14.8 %copy-start.16 = (f32[1024,256]{1,0:T(8,128)S(1)}, f32[1024,256]{1,0:T(8,128)}, u32[]{:S(2)}) copy-start(f32[1024,256]{1,0:T(8,128)} %get-tuple-element.358) | copy-start | bytes 3145732
  314.8 14.8 %copy-start.39 = (f32[1024]{0:T(1024)S(1)}, f32[1024]{0:T(1024)}, u32[]{:S(2)}) copy-start(f32[1024]{0:T(1024)} %get-tuple-element.386) | copy-start | bytes 12292
  334.9 93.8 %reduce-scatter.22.cloned.1.call-start = ((), (), s32[]{:S(2)}) async-start(), calls=%async_computation.18 | async-start | bytes 442368
  339.5 28.8 %copy-start.60 = (f32[1024]{0:T(1024)S(1)}, f32[1024]{0:T(1024)}, u32[]{:S(2)}) copy-start(f32[1024]{0:T(1024)} %get-tuple-element.382) | copy-start | bytes 12292
  339.5 28.8 %copy-start.74 = (f32[768]{0:T(1024)S(1)}, f32[768]{0:T(1024)}, u32[]{:S(2)}) copy-start(f32[768]{0:T(1024)} %param.38) | copy-start | bytes 9220
  341.3 101.1 %all-reduce.26.cloned.1.call-start = ((), (), s32[]{:S(2)}) async-start(), calls=%async_computation.16 | async-start | bytes 196608 | tf_op jit(solution)/shard_map/psum | solution.py:279
  368.2 119.7 %reduce-scatter.20.cloned.1.call-start = ((), (), s32[]{:S(2)}) async-start(), calls=%async_computation.17 | async-start | bytes 2654208 | tf_op jit(solution)/shard_map/reduce_scatter | solution.py:254
  375.3 158.3 %reduce-scatter.14.cloned.1.call-start = ((), (), s32[]{:S(2)}) async-start(), calls=%async_computation.13 | async-start | bytes 2654208 | tf_op jit(solution)/shard_map/reduce_scatter | solution.py:242
  380.9 198.2 %reduce-scatter.16.cloned.1.call-start = ((), (), s32[]{:S(2)}) async-start(), calls=%async_computation.14 | async-start | bytes 2654208 | tf_op jit(solution)/shard_map/reduce_scatter | solution.py:245
  390.8 10.8 %copy-start.48 = (f32[768]{0:T(1024)S(1)}, f32[768]{0:T(1024)}, u32[]{:S(2)}) copy-start(f32[768]{0:T(1024)} %get-tuple-element.299) | copy-start | bytes 9220
  390.8 10.8 %copy-start.50 = (f32[768]{0:T(1024)S(1)}, f32[768]{0:T(1024)}, u32[]{:S(2)}) copy-start(f32[768]{0:T(1024)} %get-tuple-element.300) | copy-start | bytes 9220
  390.9 10.8 %copy-start.52 = (f32[768]{0:T(1024)S(1)}, f32[768]{0:T(1024)}, u32[]{:S(2)}) copy-start(f32[768]{0:T(1024)} %get-tuple-element.301) | copy-start | bytes 9220
  390.9 10.8 %copy-start.54 = (f32[768]{0:T(1024)S(1)}, f32[768]{0:T(1024)}, u32[]{:S(2)}) copy-start(f32[768]{0:T(1024)} %get-tuple-element.302) | copy-start | bytes 9220
  409.2 232.7 %reduce-scatter.12.cloned.1.call-start = ((), (), s32[]{:S(2)}) async-start(), calls=%async_computation.12 | async-start | bytes 3932160 | tf_op jit(solution)/shard_map/reduce_scatter | solution.py:230
  420.0 284.8 %reduce-scatter.10.cloned.1.call-start = ((), (), s32[]{:S(2)}) async-start(), calls=%async_computation.10 | async-start | bytes 3932160 | tf_op jit(solution)/shard_map/reduce_scatter | solution.py:201
  427.8 214.1 %copy-start.6 = (bf16[256,1536]{1,0:T(8,128)(2,1)S(1)}, bf16[256,1536]{1,0:T(8,128)(2,1)}, u32[]{:S(2)}) copy-start(bf16[256,1536]{1,0:T(8,128)(2,1)} %param.22) | copy-start | bytes 2359300
  427.8 214.1 %copy-start.40 = (f32[1536]{0:T(1024)S(1)}, f32[1536]{0:T(1024)}, u32[]{:S(2)}) copy-start(f32[1536]{0:T(1024)} %param.26) | copy-start | bytes 18436
  427.8 214.1 %copy-start.58 = (f32[256]{0:T(256)S(1)}, f32[256]{0:T(256)}, u32[]{:S(2)}) copy-start(f32[256]{0:T(256)} %copy-done.57) | copy-start | bytes 3076
  427.8 215.6 %copy-start.76 = (f32[768]{0:T(1024)S(1)}, f32[768]{0:T(1024)}, u32[]{:S(2)}) copy-start(f32[768]{0:T(1024)} %get-tuple-element.283) | copy-start | bytes 9220
  427.8 277.0 %copy-start.18 = (bf16[256,1536]{1,0:T(8,128)(2,1)S(1)}, bf16[256,1536]{1,0:T(8,128)(2,1)}, u32[]{:S(2)}) copy-start(bf16[256,1536]{1,0:T(8,128)(2,1)} %param.23) | copy-start | bytes 2359300
  427.9 277.0 %copy-start.75 = (f32[256]{0:T(256)S(1)}, f32[256]{0:T(256)}, u32[]{:S(2)}) copy-start(f32[256]{0:T(256)} %get-tuple-element.391) | copy-start | bytes 3076
  (54 other events, 173.0 us)
Sparse Core Ops, SparseCore 0:
  10.0 32.9 all-gather.5
  44.8 29.7 all-gather.7
  76.5 28.8 all-gather.9
  106.9 63.4 all-gather.11
  335.1 33.0 reduce-scatter.17
  371.6 33.8 reduce-scatter.21
  407.9 34.4 all-reduce.25
  445.7 42.0 reduce-scatter.19
  491.2 42.3 reduce-scatter.13
  536.7 42.3 reduce-scatter.15
  581.4 60.3 reduce-scatter.11
  644.0 60.7 reduce-scatter.9
